TPU v7x, 32 devices: a whole 2x2x4 slice. The times are simulated.
32 devices in a mesh: dp: 4 (over x, core), space: 8 (over z, y).
Axes of the slice: x: 2, y: 2, z: 4, core: 2. Of those that a mesh axis runs over, the one named last changes fastest.
Arguments:
- section_three: bfloat16 [4, 64, 128, 512], P('dp', 'space'), parts along dimension 0, may hold values from -6 to 6
- section_four: bfloat16 [4, 32, 64, 1024], P('dp', 'space'), parts along dimension 0, may hold values from -6 to 6
- section_five: bfloat16 [4, 16, 32, 2048], P('dp', 'space'), parts along dimension 0, may hold values from -6 to 6
- lateral_three: bfloat16 [512, 256], P('space'), may hold values from -0.25 to 0.25
- lateral_four: bfloat16 [1024, 256], P('space'), may hold values from -0.1875 to 0.1875
- lateral_five: bfloat16 [2048, 256], P('space'), may hold values from -0.125 to 0.125
- lateral_bias_three: float32 [256], replicated, may hold values from -3 to 3
- lateral_bias_four: float32 [256], replicated, may hold values from -3 to 3
- lateral_bias_five: float32 [256], replicated, may hold values from -3 to 3
- output_three: bfloat16 [3, 3, 256, 256], P(None, None, 'space'), may hold values from -0.125 to 0.125
- output_four: bfloat16 [3, 3, 256, 256], P(None, None, 'space'), may hold values from -0.125 to 0.125
- output_five: bfloat16 [3, 3, 256, 256], P(None, None, 'space'), may hold values from -0.125 to 0.125
- output_bias_three: float32 [256], replicated, may hold values from -3 to 3
- output_bias_four: float32 [256], replicated, may hold values from -3 to 3
- output_bias_five: float32 [256], replicated, may hold values from -3 to 3
Outputs:
- level_three: bfloat16 [4, 64, 128, 256], P('dp', 'space'), parts along dimension 0
- level_four: bfloat16 [4, 32, 64, 256], P('dp', 'space'), parts along dimension 0
- level_five: bfloat16 [4, 16, 32, 256], P('dp'), parts along dimension 0
- level_six: bfloat16 [4, 8, 16, 256], P('dp'), parts along dimension 0
There are 4 independent parts, one for each index of `dp`. A program takes and returns all parts, laid end to end along the dimension named above; an argument that names none is the same for every part. Nothing has to cross between parts.
All inputs are finite; a program needn't handle non-finite values.
Results may differ from a plain program's by a relative error of at most 0.0095.
Values may be sent and summed in bfloat16 or wider, within the bound.
A program may use at most 64 MiB of HBM per device.

v0:
```python
import jax
import jax.numpy as jnp
from jax import lax
from jax.sharding import PartitionSpec as P


def with_halo(cells, sides, width):
    for axis, dim in sides:
        count = lax.axis_size(axis)
        ends = count - 1
        head = lax.slice_in_dim(cells, 0, width, axis=dim)
        tail = lax.slice_in_dim(cells, cells.shape[dim] - width, cells.shape[dim], axis=dim)
        cells = jnp.concatenate(
            [
                lax.ppermute(tail, axis, [(i, (i + 1) % count) for i in range(ends)]),
                cells,
                lax.ppermute(head, axis, [((i + 1) % count, i) for i in range(ends)]),
            ],
            axis=dim,
        )
    return cells


def lateral(features, weight, offset):
    images, rows, columns, channels = features.shape
    summed = (
        jnp.dot(features.reshape(-1, channels), weight, preferred_element_type=jnp.float32) + offset
    )
    return summed.reshape(images, rows, columns, -1)


def enlarge(coarse):
    return jnp.repeat(jnp.repeat(coarse, 2, axis=1), 2, axis=2)


def conv_rows(padded, weight, offset):
    images, rows_in, columns, channels = padded.shape
    height = rows_in - 2
    framed = jnp.pad(padded, ((0, 0), (0, 0), (1, 1), (0, 0)))
    summed = jnp.zeros((images * height * columns, weight.shape[3]), jnp.float32)
    for row_off in range(3):
        for col_off in range(3):
            window = framed[:, row_off : row_off + height, col_off : col_off + columns, :].reshape(
                -1, channels
            )
            summed = summed + jnp.dot(
                window, weight[row_off, col_off], preferred_element_type=jnp.float32
            )
    return (summed + offset).reshape(images, height, columns, -1).astype(jnp.bfloat16)


def on_device(
    section_three,
    section_four,
    section_five,
    lateral_three,
    lateral_four,
    lateral_five,
    lateral_bias_three,
    lateral_bias_four,
    lateral_bias_five,
    output_three,
    output_four,
    output_five,
    output_bias_three,
    output_bias_four,
    output_bias_five,
):
    whole_lat3, whole_lat4, whole_lat5, whole_out3, whole_out4, whole_out5 = (
        lax.all_gather(lateral_three, "space", axis=0, tiled=True),
        lax.all_gather(lateral_four, "space", axis=0, tiled=True),
        lax.all_gather(lateral_five, "space", axis=0, tiled=True),
        lax.all_gather(output_three, "space", axis=2, tiled=True),
        lax.all_gather(output_four, "space", axis=2, tiled=True),
        lax.all_gather(output_five, "space", axis=2, tiled=True),
    )
    merged_five = lateral(section_five, whole_lat5, lateral_bias_five).astype(jnp.bfloat16)
    merged_four = (
        lateral(section_four, whole_lat4, lateral_bias_four)
        + enlarge(merged_five).astype(jnp.float32)
    ).astype(jnp.bfloat16)
    merged_three = (
        lateral(section_three, whole_lat3, lateral_bias_three)
        + enlarge(merged_four).astype(jnp.float32)
    ).astype(jnp.bfloat16)
    rimmed_three = with_halo(merged_three, (("space", 1),), 1)
    rimmed_four = with_halo(merged_four, (("space", 1),), 1)
    level_three = conv_rows(rimmed_three, whole_out3, output_bias_three)
    level_four = conv_rows(rimmed_four, whole_out4, output_bias_four)
    whole_five = lax.all_gather(merged_five, "space", axis=1, tiled=True)
    padded_five = jnp.pad(whole_five, ((0, 0), (1, 1), (0, 0), (0, 0)))
    level_five = conv_rows(padded_five, whole_out5, output_bias_five)
    level_six = level_five[:, ::2, ::2, :]
    return (level_three, level_four, level_five, level_six)


def solution(mesh):
    return jax.shard_map(
        on_device,
        mesh=mesh,
        in_specs=(
            P("dp", "space", None, None),
            P("dp", "space", None, None),
            P("dp", "space", None, None),
            P("space", None),
            P("space", None),
            P("space", None),
            P(),
            P(),
            P(),
            P(None, None, "space", None),
            P(None, None, "space", None),
            P(None, None, "space", None),
            P(),
            P(),
            P(),
        ),
        out_specs=(
            P("dp", "space", None, None),
            P("dp", "space", None, None),
            P("dp", None, None, None),
            P("dp", None, None, None),
        ),
        check_vma=False,
    )
```

profile of v0, /device:TPU:0, one launch (start us, length us, event | category | flops | bytes accessed | tf_op | source)
XLA Modules:
  0.0 203.1 jit_solution(6566703507592191311)
XLA Ops:
  10.0 33.9 %all_gather.22 = bf16[1024,256]{1,0:T(8,128)(2,1)S(1)} all-gather(bf16[128,256]{1,0:T(8,128)(2,1)} %param.19), channel_id=1, replica_groups=mesh['dp'=4,'space'=8] {'space'}, dimensions={0}, use_global_device_ids=true | all-gather | bytes 589824 | tf_op jit(solution)/shard_map/all_gather | solution.py:71
  43.9 30.8 %all_gather.21 = bf16[512,256]{1,0:T(8,128)(2,1)S(1)} all-gather(bf16[64,256]{1,0:T(8,128)(2,1)S(1)} %copy-done.36), channel_id=1, replica_groups=mesh['dp'=4,'space'=8] {'space'}, dimensions={0}, use_global_device_ids=true | all-gather | bytes 294912 | tf_op jit(solution)/shard_map/all_gather | solution.py:70
  76.0 1.5 fusion.9
  79.4 4.7 %collective-permute-start.2 = (bf16[1,1,64,256]{3,2,1,0:T(8,128)(2,1)}, bf16[1,1,64,256]{3,2,1,0:T(8,128)(2,1)}, u32[]{:S(2)}, u32[]{:S(2)}) collective-permute-start(bf16[1,1,64,256]{3,2,1,0:T(8,128)(2,1)} %get-tuple-element.30), channel_id=1, source_target_pairs={{0,1},{1,2},{2,3},{3,4},{4,5},{5,6},{6,7},{8,9},{9,10},{10,11},{11... | collective-permute-start | bytes 98312 | tf_op jit(solution)/shard_map/ppermute | solution.py:15
  84.1 1.3 collective-permute-start.3
  85.8 1.7 convert_element_type.169
  87.6 1.3 add_convert_fusion.1
  90.4 5.2 %collective-permute-start = (bf16[1,1,128,256]{3,2,1,0:T(8,128)(2,1)}, bf16[1,1,128,256]{3,2,1,0:T(8,128)(2,1)}, u32[]{:S(2)}, u32[]{:S(2)}) collective-permute-start(bf16[1,1,128,256]{3,2,1,0:T(8,128)(2,1)} %get-tuple-element.12), channel_id=1, source_target_pairs={{0,1},{1,2},{2,3},{3,4},{4,5},{5,6},{6,7},{8,9},{9,10},{10,11},{11... | collective-permute-start | bytes 196616 | tf_op jit(solution)/shard_map/ppermute | solution.py:15
  95.6 1.3 collective-permute-start.1
  96.8 31.6 %all_gather.26 = bf16[1,16,32,256]{3,2,0,1:T(8,128)(2,1)S(1)} all-gather(bf16[1,2,32,256]{3,2,0,1:T(8,128)(2,1)S(1)} %bitcast.189), channel_id=1, replica_groups=mesh['dp'=4,'space'=8] {'space'}, dimensions={1}, use_global_device_ids=true | all-gather | bytes 294912 | tf_op jit(solution)/shard_map/all_gather | solution.py:90
  128.5 1.3 pad_slice_fusion
  130.7 1.9 convert_element_type.177
  132.6 1.7 convert_element_type.171
  136.1 1.5 pad_maximum_fusion.2
  138.7 1.6 fusion.27
  140.3 1.9 pad_maximum_fusion
  142.2 1.3 fusion.22
  143.6 1.2 convolution_add_fusion.15
  147.5 2.5 %slice.239 = bf16[1,8,16,256]{3,2,1,0:T(8,128)(2,1)} slice(bf16[1,16,32,256]{3,2,1,0:T(8,128)(2,1)S(1)} %bitcast.186), slice={[0:1:1], [0:16:2], [0:32:2], [0:256:1]} | slice | bytes 131072 | tf_op jit(solution)/shard_map/slice | solution.py:93
  150.1 1.1 fusion.24
  151.2 1.8 fusion.23
  153.1 30.5 %all-gather.7.cloned.1.call-done = bf16[3,3,256,256]{3,2,1,0:T(8,128)(2,1)} async-done(((bf16[3,3,32,256]{3,2,1,0:T(8,128)(2,1)}), bf16[3,3,256,256]{3,2,1,0:T(8,128)(2,1)}) %all-gather.7.cloned.1.call-update) | async-done | bytes 1179664 | tf_op jit(solution)/shard_map/all_gather | solution.py:73
  183.5 1.3 fusion.26
  195.5 1.1 fusion.3
  (139 shorter events, 24.6 us)
Async XLA Ops:
  7.2 67.8 %copy-start = (bf16[1,8,128,512]{3,2,1,0:T(8,128)(2,1)S(1)}, bf16[1,8,128,512]{3,2,1,0:T(8,128)(2,1)}, u32[]{:S(2)}) copy-start(bf16[1,8,128,512]{3,2,1,0:T(8,128)(2,1)} %param.15) | copy-start | bytes 3145732
  7.2 36.7 %copy-start.36 = (bf16[64,256]{1,0:T(8,128)(2,1)S(1)}, bf16[64,256]{1,0:T(8,128)(2,1)}, u32[]{:S(2)}) copy-start(bf16[64,256]{1,0:T(8,128)(2,1)} %param.18) | copy-start | bytes 98308
  7.2 67.5 %copy-start.24 = (bf16[1,4,64,1024]{3,2,1,0:T(8,128)(2,1)S(1)}, bf16[1,4,64,1024]{3,2,1,0:T(8,128)(2,1)}, u32[]{:S(2)}) copy-start(bf16[1,4,64,1024]{3,2,1,0:T(8,128)(2,1)} %param.16) | copy-start | bytes 1572868
  7.2 67.5 %copy-start.40 = (f32[256]{0:T(256)S(1)}, f32[256]{0:T(256)}, u32[]{:S(2)}) copy-start(f32[256]{0:T(256)} %param.22) | copy-start | bytes 3076
  7.2 68.3 %all-gather.5.cloned.1.call-start = ((), (), s32[]{:S(2)}) async-start(), calls=%async_computation | async-start | bytes 1179648 | tf_op jit(solution)/shard_map/all_gather | solution.py:72
  7.9 134.3 %all-gather.11.cloned.1.call-start = ((), (), s32[]{:S(2)}) async-start(), calls=%async_computation.3 | async-start | bytes 1327104 | tf_op jit(solution)/shard_map/all_gather | solution.py:75
  8.7 141.4 %all-gather.9.cloned.1.call-start = ((), (), s32[]{:S(2)}) async-start(), calls=%async_computation.2 | async-start | bytes 1327104 | tf_op jit(solution)/shard_map/all_gather | solution.py:74
  9.4 65.6 %copy-start.37 = (f32[256]{0:T(256)S(1)}, f32[256]{0:T(256)}, u32[]{:S(2)}) copy-start(f32[256]{0:T(256)} %param.21) | copy-start | bytes 3076
  9.4 174.1 %all-gather.7.cloned.1.call-start = ((), (), s32[]{:S(2)}) async-start(), calls=%async_computation.1 | async-start | bytes 1327104 | tf_op jit(solution)/shard_map/all_gather | solution.py:73
  75.0 10.4 %copy-start.4 = (f32[256,256]{1,0:T(8,128)}, f32[256,256]{1,0:T(8,128)S(1)}, u32[]{:S(2)}) copy-start(f32[256,256]{1,0:T(8,128)S(1)} %convolution_add_fusion.23) | copy-start | bytes 786436
  78.3 7.1 %copy-start.3 = (f32[4,32,2,256]{3,2,1,0:T(2,128)}, f32[4,32,2,256]{3,2,1,0:T(2,128)S(1)}, u32[]{:S(2)}) copy-start(f32[4,32,2,256]{3,2,1,0:T(2,128)S(1)} %broadcast_in_dim.9) | copy-start | bytes 786436
  79.4 55.0 %collective-permute-start.2 = (bf16[1,1,64,256]{3,2,1,0:T(8,128)(2,1)}, bf16[1,1,64,256]{3,2,1,0:T(8,128)(2,1)}, u32[]{:S(2)}, u32[]{:S(2)}) collective-permute-start(bf16[1,1,64,256]{3,2,1,0:T(8,128)(2,1)} %get-tuple-element.30), channel_id=1, source_target_pairs={{0,1},{1,2},{2,3},{3,4},{4,5},{5,6},{6,7},{8,9},{9,10},{10,11},{11... | collective-permute-start | bytes 98312 | tf_op jit(solution)/shard_map/ppermute | solution.py:15
  84.1 50.2 %collective-permute-start.3 = (bf16[1,1,64,256]{3,2,1,0:T(8,128)(2,1)}, bf16[1,1,64,256]{3,2,1,0:T(8,128)(2,1)}, u32[]{:S(2)}, u32[]{:S(2)}) collective-permute-start(bf16[1,1,64,256]{3,2,1,0:T(8,128)(2,1)} %get-tuple-element.31), channel_id=1, source_target_pairs={{1,0},{2,1},{3,2},{4,3},{5,4},{6,5},{7,6},{9,8},{10,9},{11,10},{12... | collective-permute-start | bytes 98312 | tf_op jit(solution)/shard_map/ppermute | solution.py:17
  87.6 9.3 %copy-start.34 = (bf16[64,256]{1,0:T(8,128)(2,1)S(1)}, bf16[64,256]{1,0:T(8,128)(2,1)}, u32[]{:S(2)}) copy-start(bf16[64,256]{1,0:T(8,128)(2,1)} %copy-done.33) | copy-start | bytes 98308
  90.4 47.2 %collective-permute-start = (bf16[1,1,128,256]{3,2,1,0:T(8,128)(2,1)}, bf16[1,1,128,256]{3,2,1,0:T(8,128)(2,1)}, u32[]{:S(2)}, u32[]{:S(2)}) collective-permute-start(bf16[1,1,128,256]{3,2,1,0:T(8,128)(2,1)} %get-tuple-element.12), channel_id=1, source_target_pairs={{0,1},{1,2},{2,3},{3,4},{4,5},{5,6},{6,7},{8,9},{9,10},{10,11},{11... | collective-permute-start | bytes 196616 | tf_op jit(solution)/shard_map/ppermute | solution.py:15
  95.6 42.1 %collective-permute-start.1 = (bf16[1,1,128,256]{3,2,1,0:T(8,128)(2,1)}, bf16[1,1,128,256]{3,2,1,0:T(8,128)(2,1)}, u32[]{:S(2)}, u32[]{:S(2)}) collective-permute-start(bf16[1,1,128,256]{3,2,1,0:T(8,128)(2,1)} %get-tuple-element.13), channel_id=1, source_target_pairs={{1,0},{2,1},{3,2},{4,3},{5,4},{6,5},{7,6},{9,8},{10,9},{11,10},{12... | collective-permute-start | bytes 196616 | tf_op jit(solution)/shard_map/ppermute | solution.py:17
  134.3 3.3 %copy-start.2 = (bf16[1,8,128,256]{3,2,1,0:T(8,128)(2,1)S(1)}, bf16[1,8,128,256]{3,2,1,0:T(8,128)(2,1)}, u32[]{:S(2)}) copy-start(bf16[1,8,128,256]{3,2,1,0:T(8,128)(2,1)} %copy-done.1) | copy-start | bytes 1572868
  142.2 2.6 %copy-start.14 = (bf16[3,3,256,256]{3,2,1,0:T(8,128)(2,1)S(1)}, bf16[3,3,256,256]{3,2,1,0:T(8,128)(2,1)}, u32[]{:S(2)}) copy-start(bf16[3,3,256,256]{3,2,1,0:T(8,128)(2,1)} %all-gather.11.cloned.1.call-done) | copy-start | bytes 3538948
  142.2 2.6 %copy-start.21 = (bf16[1,16,32,256]{3,2,0,1:T(8,128)(2,1)S(1)}, bf16[1,16,32,256]{3,2,0,1:T(8,128)(2,1)}, u32[]{:S(2)}) copy-start(bf16[1,16,32,256]{3,2,0,1:T(8,128)(2,1)} %get-tuple-element.17) | copy-start | bytes 786436
  143.6 1.5 copy-start.20
  147.2 4.0 %copy-start.31 = (bf16[1,4,64,256]{3,2,1,0:T(8,128)(2,1)S(1)}, bf16[1,4,64,256]{3,2,1,0:T(8,128)(2,1)}, u32[]{:S(2)}) copy-start(bf16[1,4,64,256]{3,2,1,0:T(8,128)(2,1)} %get-tuple-element.27) | copy-start | bytes 393220
  147.5 2.6 %copy-start.32 = (bf16[512,256]{1,0:T(8,128)(2,1)}, bf16[512,256]{1,0:T(8,128)(2,1)S(1)}, u32[]{:S(2)}) copy-start(bf16[512,256]{1,0:T(8,128)(2,1)S(1)} %fusion.5) | copy-start | bytes 786436
  193.6 1.8 copy-start.11
  193.7 1.8 copy-start.39
  (27 other events, 28.3 us)
Sparse Core Ops, SparseCore 0:
  10.1 44.0 all-gather.4
  56.4 42.5 all-gather.10
  101.2 40.1 all-gather.8
  143.5 39.9 all-gather.6
where the time goes:
time: 204 us; the launch traced here: 203 us
  blocking collectives  96.2 us (47%)
  waiting for transfers between devices  33.1 us (16%)
  local copies, waits for them, and re-layouts  24.3 us (12%)
  matrix products  15.8 us (8%)
  between operations  14.3 us (7%)
  starting transfers between devices  12.6 us (6%)
  other arithmetic  6.78 us (3%)
    all_gather x1, blocking collectives, on_device(): lax.all_gather(lateral_four, 'space', axis=0, tiled=True)  33.9 us
    all_gather x1, blocking collectives, on_device(): whole_five = lax.all_gather(merged_five, 'space', axis=1, tiled=True)  31.6 us
    all_gather x1, blocking collectives, on_device(): lax.all_gather(lateral_three, 'space', axis=0, tiled=True)  30.8 us
    all_gather x1, waiting for transfers between devices, on_device(): lax.all_gather(output_three, 'space', axis=2, tiled=True)  30.5 us
    dot_general x27, matrix products, conv_rows(): jnp.dot(window, weight[row_off, col_off], preferred_element_type=jnp.floa...  13.5 us
    ppermute x2, starting transfers between devices, with_halo(): lax.ppermute(tail, axis, [(i, (i + 1) % count) for i in range(ends)])  9.9 us
    unnamed x86, local copies, waits for them, and re-layouts  9.46 us
    concatenate x4, other arithmetic, with_halo(): jnp.concatenate([lax.ppermute(tail, axis, [(i, (i + 1) % count) for i in...  5.37 us
  transfers between devices with their start and end apart: 8, of which 1 were waited for; matrix products, arithmetic and copies ran while one was open for 15% of the time, Pallas kernels for 0%

commit v1 on v0

--- a/solution.py
+++ b/solution.py
@@ -2,6 +2,11 @@
 import jax.numpy as jnp
 from jax import lax
 from jax.sharding import PartitionSpec as P
+
+
+def all_parts(x, mesh_axis, dim):
+    shards = lax.all_gather(x, mesh_axis)
+    return jnp.concatenate(shards, axis=dim)
 
 
 def with_halo(cells, sides, width):
@@ -70,7 +75,7 @@
         lax.all_gather(lateral_three, "space", axis=0, tiled=True),
         lax.all_gather(lateral_four, "space", axis=0, tiled=True),
         lax.all_gather(lateral_five, "space", axis=0, tiled=True),
-        lax.all_gather(output_three, "space", axis=2, tiled=True),
+        all_parts(output_three, "space", 2),
         lax.all_gather(output_four, "space", axis=2, tiled=True),
         lax.all_gather(output_five, "space", axis=2, tiled=True),
     )

time: 204 us -> 197 us (0.966)
  waiting for transfers between devices: 33.1 us -> 26.1 us
    all_gather x1, waiting for transfers between devices: 30.5 us -> 0.01 us  [all_parts(): shards = lax.all_gather(x, mesh_axis)]
    all_gather x1, waiting for transfers between devices: 0.01 us -> 21.7 us  [on_device(): lax.all_gather(output_four, 'space', axis=2, tiled=True)]
    unnamed x86 -> x84, local copies, waits for them, and re-layouts: 9.46 us -> 7.63 us
  transfers between devices with their start and end apart: 8 -> 8, of which waited for: 1 -> 2; matrix products, arithmetic and copies ran while one was open for 15% -> 17% of each run, Pallas kernels for 0% -> 0%
where the time goes in v1:
time: 197 us; the launch traced here: 196 us
  blocking collectives  95.5 us (48%)
  waiting for transfers between devices  26.1 us (13%)
  local copies, waits for them, and re-layouts  23.9 us (12%)
  matrix products  16.2 us (8%)
  between operations  14.4 us (7%)
  starting transfers between devices  12.7 us (6%)
  other arithmetic  6.64 us (3%)
    all_gather x1, blocking collectives, on_device(): lax.all_gather(lateral_four, 'space', axis=0, tiled=True)  33.9 us
    all_gather x1, blocking collectives, on_device(): whole_five = lax.all_gather(merged_five, 'space', axis=1, tiled=True)  30.9 us
    all_gather x1, blocking collectives, on_device(): lax.all_gather(lateral_three, 'space', axis=0, tiled=True)  30.8 us
    all_gather x1, waiting for transfers between devices, on_device(): lax.all_gather(output_four, 'space', axis=2, tiled=True)  21.7 us
    dot_general x27, matrix products, conv_rows(): jnp.dot(window, weight[row_off, col_off], preferred_element_type=jnp.floa...  14 us
    ppermute x2, starting transfers between devices, with_halo(): lax.ppermute(tail, axis, [(i, (i + 1) % count) for i in range(ends)])  9.87 us
    unnamed x84, local copies, waits for them, and re-layouts  7.63 us
    concatenate x4, other arithmetic, with_halo(): jnp.concatenate([lax.ppermute(tail, axis, [(i, (i + 1) % count) for i in...  5.23 us
  transfers between devices with their start and end apart: 8, of which 2 were waited for; matrix products, arithmetic and copies ran while one was open for 17% of the time, Pallas kernels for 0%

profile of v1, /device:TPU:0, one launch (start us, length us, event | category | flops | bytes accessed | tf_op | source)
XLA Modules:
  0.0 195.5 jit_solution(2938980113236783174)
XLA Ops:
  10.0 33.9 %all_gather.25 = bf16[1024,256]{1,0:T(8,128)(2,1)S(1)} all-gather(bf16[128,256]{1,0:T(8,128)(2,1)} %param.19), channel_id=1, replica_groups=mesh['dp'=4,'space'=8] {'space'}, dimensions={0}, use_global_device_ids=true | all-gather | bytes 589824 | tf_op jit(solution)/shard_map/all_gather | solution.py:76
  43.9 30.8 %all_gather.24 = bf16[512,256]{1,0:T(8,128)(2,1)S(1)} all-gather(bf16[64,256]{1,0:T(8,128)(2,1)S(1)} %copy-done.35), channel_id=1, replica_groups=mesh['dp'=4,'space'=8] {'space'}, dimensions={0}, use_global_device_ids=true | all-gather | bytes 294912 | tf_op jit(solution)/shard_map/all_gather | solution.py:75
  76.0 1.5 fusion.9
  78.7 4.7 %collective-permute-start.2 = (bf16[1,1,64,256]{3,2,1,0:T(8,128)(2,1)}, bf16[1,1,64,256]{3,2,1,0:T(8,128)(2,1)}, u32[]{:S(2)}, u32[]{:S(2)}) collective-permute-start(bf16[1,1,64,256]{3,2,1,0:T(8,128)(2,1)} %get-tuple-element.30), channel_id=1, source_target_pairs={{0,1},{1,2},{2,3},{3,4},{4,5},{5,6},{6,7},{8,9},{9,10},{10,11},{11... | collective-permute-start | bytes 98312 | tf_op jit(solution)/shard_map/ppermute | solution.py:20
  83.5 1.3 collective-permute-start.3
  85.2 1.7 convert_element_type.169
  86.9 1.3 add_convert_fusion.1
  89.7 5.2 %collective-permute-start = (bf16[1,1,128,256]{3,2,1,0:T(8,128)(2,1)}, bf16[1,1,128,256]{3,2,1,0:T(8,128)(2,1)}, u32[]{:S(2)}, u32[]{:S(2)}) collective-permute-start(bf16[1,1,128,256]{3,2,1,0:T(8,128)(2,1)} %get-tuple-element.12), channel_id=1, source_target_pairs={{0,1},{1,2},{2,3},{3,4},{4,5},{5,6},{6,7},{8,9},{9,10},{10,11},{11... | collective-permute-start | bytes 196616 | tf_op jit(solution)/shard_map/ppermute | solution.py:20
  94.9 30.9 %all_gather.30 = bf16[1,16,32,256]{3,2,0,1:T(8,128)(2,1)S(1)} all-gather(bf16[1,2,32,256]{3,2,0,1:T(8,128)(2,1)S(1)} %bitcast.203), channel_id=1, replica_groups=mesh['dp'=4,'space'=8] {'space'}, dimensions={1}, use_global_device_ids=true | all-gather | bytes 294912 | tf_op jit(solution)/shard_map/all_gather | solution.py:95
  125.8 1.3 pad_slice_fusion
  128.0 1.8 convert_element_type.177
  129.8 1.7 convert_element_type.171
  131.5 1.4 collective-permute-start.1
  134.7 1.5 pad_maximum_fusion.2
  136.2 1.8 collective-permute-done.1
  139.0 1.8 fusion.27
  140.9 1.9 pad_maximum_fusion
  142.7 1.4 copy.20
  144.2 1.3 fusion.22
  145.5 1.2 convolution_add_fusion.15
  149.4 2.5 %slice.239 = bf16[1,8,16,256]{3,2,1,0:T(8,128)(2,1)} slice(bf16[1,16,32,256]{3,2,1,0:T(8,128)(2,1)S(1)} %bitcast.200), slice={[0:1:1], [0:16:2], [0:32:2], [0:256:1]} | slice | bytes 131072 | tf_op jit(solution)/shard_map/slice | solution.py:98
  152.0 1.4 fusion.26
  161.3 21.7 %all-gather.8.cloned.1.call-done = bf16[3,3,256,256]{3,2,1,0:T(8,128)(2,1)} async-done(((bf16[3,3,32,256]{3,2,1,0:T(8,128)(2,1)}), bf16[3,3,256,256]{3,2,1,0:T(8,128)(2,1)}) %all-gather.8.cloned.1.call-update) | async-done | bytes 1179664 | tf_op jit(solution)/shard_map/all_gather | solution.py:79
  185.3 1.2 convolution_add_fusion.22
  (138 shorter events, 25.8 us)
Async XLA Ops:
  7.2 67.8 %copy-start = (bf16[1,8,128,512]{3,2,1,0:T(8,128)(2,1)S(1)}, bf16[1,8,128,512]{3,2,1,0:T(8,128)(2,1)}, u32[]{:S(2)}) copy-start(bf16[1,8,128,512]{3,2,1,0:T(8,128)(2,1)} %param.15) | copy-start | bytes 3145732
  7.2 36.7 %copy-start.35 = (bf16[64,256]{1,0:T(8,128)(2,1)S(1)}, bf16[64,256]{1,0:T(8,128)(2,1)}, u32[]{:S(2)}) copy-start(bf16[64,256]{1,0:T(8,128)(2,1)} %param.18) | copy-start | bytes 98308
  7.2 67.5 %copy-start.23 = (bf16[1,4,64,1024]{3,2,1,0:T(8,128)(2,1)S(1)}, bf16[1,4,64,1024]{3,2,1,0:T(8,128)(2,1)}, u32[]{:S(2)}) copy-start(bf16[1,4,64,1024]{3,2,1,0:T(8,128)(2,1)} %param.16) | copy-start | bytes 1572868
  7.2 67.4 %copy-start.39 = (f32[256]{0:T(256)S(1)}, f32[256]{0:T(256)}, u32[]{:S(2)}) copy-start(f32[256]{0:T(256)} %param.22) | copy-start | bytes 3076
  7.2 68.3 %all-gather.6.cloned.1.call-start = ((), (), s32[]{:S(2)}) async-start(), calls=%async_computation | async-start | bytes 1179648 | tf_op jit(solution)/shard_map/all_gather | solution.py:77
  7.9 134.8 %all-gather.12.cloned.1.call-start = ((), (), s32[]{:S(2)}) async-start(), calls=%async_computation.3 | async-start | bytes 1327104 | tf_op jit(solution)/shard_map/all_gather | solution.py:8
  8.7 135.4 %all-gather.10.cloned.1.call-start = ((), (), s32[]{:S(2)}) async-start(), calls=%async_computation.2 | async-start | bytes 1327104 | tf_op jit(solution)/shard_map/all_gather | solution.py:80
  9.4 65.6 %copy-start.36 = (f32[256]{0:T(256)S(1)}, f32[256]{0:T(256)}, u32[]{:S(2)}) copy-start(f32[256]{0:T(256)} %param.21) | copy-start | bytes 3076
  9.4 173.5 %all-gather.8.cloned.1.call-start = ((), (), s32[]{:S(2)}) async-start(), calls=%async_computation.1 | async-start | bytes 1327104 | tf_op jit(solution)/shard_map/all_gather | solution.py:79
  75.0 9.8 %copy-start.4 = (f32[256,256]{1,0:T(8,128)}, f32[256,256]{1,0:T(8,128)S(1)}, u32[]{:S(2)}) copy-start(f32[256,256]{1,0:T(8,128)S(1)} %convolution_add_fusion.23) | copy-start | bytes 786436
  77.7 7.1 %copy-start.3 = (f32[4,32,2,256]{3,2,1,0:T(2,128)}, f32[4,32,2,256]{3,2,1,0:T(2,128)S(1)}, u32[]{:S(2)}) copy-start(f32[4,32,2,256]{3,2,1,0:T(2,128)S(1)} %broadcast_in_dim.9) | copy-start | bytes 786436
  78.7 54.2 %collective-permute-start.2 = (bf16[1,1,64,256]{3,2,1,0:T(8,128)(2,1)}, bf16[1,1,64,256]{3,2,1,0:T(8,128)(2,1)}, u32[]{:S(2)}, u32[]{:S(2)}) collective-permute-start(bf16[1,1,64,256]{3,2,1,0:T(8,128)(2,1)} %get-tuple-element.30), channel_id=1, source_target_pairs={{0,1},{1,2},{2,3},{3,4},{4,5},{5,6},{6,7},{8,9},{9,10},{10,11},{11... | collective-permute-start | bytes 98312 | tf_op jit(solution)/shard_map/ppermute | solution.py:20
  83.5 49.5 %collective-permute-start.3 = (bf16[1,1,64,256]{3,2,1,0:T(8,128)(2,1)}, bf16[1,1,64,256]{3,2,1,0:T(8,128)(2,1)}, u32[]{:S(2)}, u32[]{:S(2)}) collective-permute-start(bf16[1,1,64,256]{3,2,1,0:T(8,128)(2,1)} %get-tuple-element.31), channel_id=1, source_target_pairs={{1,0},{2,1},{3,2},{4,3},{5,4},{6,5},{7,6},{9,8},{10,9},{11,10},{12... | collective-permute-start | bytes 98312 | tf_op jit(solution)/shard_map/ppermute | solution.py:22
  86.9 8.0 %copy-start.33 = (bf16[64,256]{1,0:T(8,128)(2,1)S(1)}, bf16[64,256]{1,0:T(8,128)(2,1)}, u32[]{:S(2)}) copy-start(bf16[64,256]{1,0:T(8,128)(2,1)} %copy-done.32) | copy-start | bytes 98308
  89.7 46.5 %collective-permute-start = (bf16[1,1,128,256]{3,2,1,0:T(8,128)(2,1)}, bf16[1,1,128,256]{3,2,1,0:T(8,128)(2,1)}, u32[]{:S(2)}, u32[]{:S(2)}) collective-permute-start(bf16[1,1,128,256]{3,2,1,0:T(8,128)(2,1)} %get-tuple-element.12), channel_id=1, source_target_pairs={{0,1},{1,2},{2,3},{3,4},{4,5},{5,6},{6,7},{8,9},{9,10},{10,11},{11... | collective-permute-start | bytes 196616 | tf_op jit(solution)/shard_map/ppermute | solution.py:20
  131.5 6.5 %copy-start.2 = (bf16[1,8,128,256]{3,2,1,0:T(8,128)(2,1)S(1)}, bf16[1,8,128,256]{3,2,1,0:T(8,128)(2,1)}, u32[]{:S(2)}) copy-start(bf16[1,8,128,256]{3,2,1,0:T(8,128)(2,1)} %copy-done.1) | copy-start | bytes 1572868
  131.5 6.5 %collective-permute-start.1 = (bf16[1,1,128,256]{3,2,1,0:T(8,128)(2,1)}, bf16[1,1,128,256]{3,2,1,0:T(8,128)(2,1)S(1)}, u32[]{:S(2)}, u32[]{:S(2)}) collective-permute-start(bf16[1,1,128,256]{3,2,1,0:T(8,128)(2,1)} %get-tuple-element.13), channel_id=1, source_target_pairs={{1,0},{2,1},{3,2},{4,3},{5,4},{6,5},{7,6},{9,8},{10,9},{11,10},{12... | collective-permute-start | bytes 196616 | tf_op jit(solution)/shard_map/ppermute | solution.py:22
  144.1 2.6 %copy-start.15 = (bf16[3,3,256,256]{3,2,1,0:T(8,128)(2,1)S(1)}, bf16[3,3,256,256]{3,2,1,0:T(8,128)(2,1)}, u32[]{:S(2)}) copy-start(bf16[3,3,256,256]{3,2,1,0:T(8,128)(2,1)} %all-gather.10.cloned.1.call-done) | copy-start | bytes 3538948
  149.4 4.3 %copy-start.31 = (bf16[512,256]{1,0:T(8,128)(2,1)}, bf16[512,256]{1,0:T(8,128)(2,1)S(1)}, u32[]{:S(2)}) copy-start(bf16[512,256]{1,0:T(8,128)(2,1)S(1)} %fusion.5) | copy-start | bytes 786436
  160.2 22.8 %copy-start.30 = (bf16[1,4,64,256]{3,2,1,0:T(8,128)(2,1)S(1)}, bf16[1,4,64,256]{3,2,1,0:T(8,128)(2,1)}, u32[]{:S(2)}) copy-start(bf16[1,4,64,256]{3,2,1,0:T(8,128)(2,1)} %get-tuple-element.26) | copy-start | bytes 393220
  160.2 24.0 %copy-start.29 = (bf16[1,4,64,256]{3,2,1,0:T(8,128)(2,1)S(1)}, bf16[1,4,64,256]{3,2,1,0:T(8,128)(2,1)}, u32[]{:S(2)}) copy-start(bf16[1,4,64,256]{3,2,1,0:T(8,128)(2,1)} %get-tuple-element.27) | copy-start | bytes 393220
  161.3 25.3 %copy-start.28 = (bf16[1,4,64,256]{3,2,1,0:T(8,128)(2,1)S(1)}, bf16[1,4,64,256]{3,2,1,0:T(8,128)(2,1)}, u32[]{:S(2)}) copy-start(bf16[1,4,64,256]{3,2,1,0:T(8,128)(2,1)} %get-tuple-element.25) | copy-start | bytes 393220
  183.0 3.6 %copy-start.14 = (bf16[3,3,256,256]{3,2,1,0:T(8,128)(2,1)S(1)}, bf16[3,3,256,256]{3,2,1,0:T(8,128)(2,1)}, u32[]{:S(2)}) copy-start(bf16[3,3,256,256]{3,2,1,0:T(8,128)(2,1)} %all-gather.8.cloned.1.call-done) | copy-start | bytes 3538948
  184.2 2.6 %copy-start.27 = (bf16[1,4,64,256]{3,2,1,0:T(8,128)(2,1)S(1)}, bf16[1,4,64,256]{3,2,1,0:T(8,128)(2,1)}, u32[]{:S(2)}) copy-start(bf16[1,4,64,256]{3,2,1,0:T(8,128)(2,1)} %get-tuple-element.24) | copy-start | bytes 393220
  (26 other events, 30.4 us)
Sparse Core Ops, SparseCore 0:
  10.1 44.0 all-gather.5
  56.4 42.2 all-gather.11
  100.9 40.0 all-gather.9
  143.0 39.8 all-gather.7
